TPU v7x, 32 devices: a whole 2x2x4 slice. The times are simulated.
32 devices in a mesh: part: 2 (over x), ray: 4 (over z), pix: 4 (over y, core).
Axes of the slice: x: 2, y: 2, z: 4, core: 2. Of those that a mesh axis runs over, the one named last changes fastest.
Arguments:
- sys_mat: bfloat16 [23040, 16384], P('ray', 'pix')
- x_init: float32 [16384, 512], P('pix', 'part'), parts along dimension 1
- sinogram: float32 [23040, 512], P('ray', 'part'), parts along dimension 1
- row_inv: float32 [23040], P('ray')
- col_inv: float32 [16384], P('pix')
- relaxation: float32 [], replicated
Outputs:
- output 1: float32 [16384, 512], P('pix', 'part'), parts along dimension 1
- output 2: float32 [23040, 512], P('ray', 'part'), parts along dimension 1
- output 3: float32 [6, 512], P(None, 'part'), parts along dimension 1
There are 2 independent parts. A program takes and returns all parts, laid end to end along the dimension named above; an argument that names none is the same for every part.
All inputs are finite; a program needn't handle non-finite values.
Results may differ from a plain program's by a relative error of at most 0.001.
Values are sent between devices in bfloat16 or wider.
A program may use at most 1 GiB of HBM per device.

v0:
```python
import jax
import jax.numpy as jnp
from jax import lax
from jax.sharding import PartitionSpec as P

SWEEPS = 6


def solution(mesh):
    ray_size = mesh.shape["ray"]

    def local_sweeps(a_blk, x_loc, sino_loc, row_inv, col_inv, relaxation):
        ray_total = a_blk.shape[0] * ray_size
        x_cur = x_loc
        sq_list = []
        residual = sino_loc
        for sweep_idx in range(SWEEPS):
            part_proj = jnp.dot(a_blk, x_cur.astype(jnp.bfloat16), preferred_element_type=jnp.float32)
            projected = lax.psum(part_proj, "pix")
            residual = row_inv[:, None] * (sino_loc - projected)
            sq_list.append(lax.psum(jnp.sum(residual * residual, axis=0), "ray") / ray_total)
            part_back = lax.dot_general(a_blk, residual.astype(jnp.bfloat16), (((0,), (0,)), ((), ())), preferred_element_type=jnp.float32)
            back_proj = lax.psum(part_back, "ray")
            x_cur = x_cur + relaxation * col_inv[:, None] * back_proj
        return x_cur, residual, jnp.stack(sq_list)

    return jax.shard_map(
        local_sweeps,
        mesh=mesh,
        in_specs=(P("ray", "pix"), P("pix", "part"), P("ray", "part"), P("ray"), P("pix"), P()),
        out_specs=(P("pix", "part"), P("ray", "part"), P(None, "part")),
        check_vma=False,
    )
```

profile of v0, /device:TPU:0, one launch (start us, length us, event | category | flops | bytes accessed | tf_op | source)
XLA Modules:
  0.0 1956.5 jit_solution(14011513552475440830)
XLA Ops:
  7.2 23.7 %fusion.11 = f32[5760,256]{1,0:T(8,128)} fusion(bf16[5760,4096]{1,0:T(8,128)(2,1)} %param.6, f32[4096,256]{1,0:T(8,128)} %param.7), kind=kOutput, calls=%fused_computation.40 | convolution fusion | flops 12080644096 | bytes 57278464 | tf_op jit(solution)/shard_map/dot_general | solution.py:18
  31.0 115.8 %all-reduce.14.cloned.1.call-done = f32[5760,256]{1,0:T(8,128)} async-done(((f32[5760,256]{1,0:T(8,128)}), f32[5760,256]{1,0:T(8,128)}) %all-reduce.14.cloned.1.call-update) | async-done | bytes 5898256 | tf_op jit(solution)/shard_map/psum | solution.py:19
  146.8 25.8 %convolution_bitcast_fusion.10 = f32[4096,256]{0,1:T(8,128)} fusion(bf16[5760,4096]{1,0:T(8,128)(2,1)} %param.6, f32[5760,256]{1,0:T(8,128)} %param.8, f32[5760,256]{1,0:T(8,128)} %all-reduce.14.cloned.1.call-done, f32[5760]{0:T(1024)S(1)} %copy-done.3), kind=kOutput, calls=%fused_computation.22 | convolution fusion | flops 12084019200 | bytes 63199744 | tf_op jit(solution)/shard_map/dot_general | solution.py:22
  172.9 5.6 copy.9
  179.2 147.7 %all-reduce.16.cloned.1.call-done = f32[4096,256]{0,1:T(8,128)} async-done(((f32[4096,256]{0,1:T(8,128)}), f32[4096,256]{0,1:T(8,128)}) %all-reduce.16.cloned.1.call-update) | async-done | bytes 4194320 | tf_op jit(solution)/shard_map/psum | solution.py:23
  326.8 25.0 %convolution_bitcast_fusion.4 = f32[5760,256]{1,0:T(8,128)} fusion(bf16[5760,4096]{1,0:T(8,128)(2,1)} %param.6, f32[4096,256]{0,1:T(8,128)} %copy.9, f32[4096,256]{0,1:T(8,128)} %all-reduce.16.cloned.1.call-done, f32[4096]{0:T(1024)S(1)} %broadcast_multiply_fusion), kind=kOutput, calls=%fused_computation.4 | convolution fusion | flops 12082741248 | bytes 61489152 | tf_op jit(solution)/shard_map/dot_general | solution.py:18
  351.9 112.1 %all-reduce.18.cloned.1.call-done = f32[5760,256]{1,0:T(8,128)} async-done(((f32[5760,256]{1,0:T(8,128)}), f32[5760,256]{1,0:T(8,128)}) %all-reduce.18.cloned.1.call-update) | async-done | bytes 5898256 | tf_op jit(solution)/shard_map/psum | solution.py:19
  464.0 25.7 %convolution_bitcast_fusion.9 = f32[4096,256]{0,1:T(8,128)} fusion(bf16[5760,4096]{1,0:T(8,128)(2,1)} %param.6, f32[5760,256]{1,0:T(8,128)} %param.8, f32[5760,256]{1,0:T(8,128)} %all-reduce.18.cloned.1.call-done, f32[5760]{0:T(1024)S(1)} %copy-done.3), kind=kOutput, calls=%fused_computation.21 | convolution fusion | flops 12084019200 | bytes 63199744 | tf_op jit(solution)/shard_map/dot_general | solution.py:22
  490.3 153.7 %all-reduce.20.cloned.1.call-done = f32[4096,256]{0,1:T(8,128)} async-done(((f32[4096,256]{0,1:T(8,128)}), f32[4096,256]{0,1:T(8,128)}) %all-reduce.20.cloned.1.call-update) | async-done | bytes 4194320 | tf_op jit(solution)/shard_map/psum | solution.py:23
  644.0 5.9 multiply_add_fusion.4
  651.9 21.5 %convolution_bitcast_fusion.3 = f32[5760,256]{1,0:T(8,128)} fusion(bf16[5760,4096]{1,0:T(8,128)(2,1)} %param.6, f32[4096,256]{0,1:T(8,128)S(1)} %multiply_add_fusion.4), kind=kOutput, calls=%fused_computation.3 | convolution fusion | flops 12080644096 | bytes 57278464 | tf_op jit(solution)/shard_map/dot_general | solution.py:18
  673.4 112.1 %all-reduce.22.cloned.1.call-done = f32[5760,256]{1,0:T(8,128)} async-done(((f32[5760,256]{1,0:T(8,128)}), f32[5760,256]{1,0:T(8,128)}) %all-reduce.22.cloned.1.call-update) | async-done | bytes 5898256 | tf_op jit(solution)/shard_map/psum | solution.py:19
  785.5 25.8 %convolution_bitcast_fusion.8 = f32[4096,256]{0,1:T(8,128)} fusion(bf16[5760,4096]{1,0:T(8,128)(2,1)} %param.6, f32[5760,256]{1,0:T(8,128)} %param.8, f32[5760,256]{1,0:T(8,128)} %all-reduce.22.cloned.1.call-done, f32[5760]{0:T(1024)S(1)} %copy-done.3), kind=kOutput, calls=%fused_computation.20 | convolution fusion | flops 12084019200 | bytes 63199744 | tf_op jit(solution)/shard_map/dot_general | solution.py:22
  811.6 154.0 %all-reduce.24.cloned.1.call-done = f32[4096,256]{0,1:T(8,128)} async-done(((f32[4096,256]{0,1:T(8,128)}), f32[4096,256]{0,1:T(8,128)}) %all-reduce.24.cloned.1.call-update) | async-done | bytes 4194320 | tf_op jit(solution)/shard_map/psum | solution.py:23
  965.6 25.0 %convolution_bitcast_fusion.2 = f32[5760,256]{1,0:T(8,128)} fusion(bf16[5760,4096]{1,0:T(8,128)(2,1)} %param.6, f32[4096,256]{0,1:T(8,128)} %copy-done.2, f32[4096,256]{0,1:T(8,128)} %all-reduce.24.cloned.1.call-done, f32[4096]{0:T(1024)S(1)} %broadcast_multiply_fusion), kind=kOutput, calls=%fused_computation.2 | convolution fusion | flops 12082741248 | bytes 61489152 | tf_op jit(solution)/shard_map/dot_general | solution.py:18
  990.7 112.1 %all-reduce.26.cloned.1.call-done = f32[5760,256]{1,0:T(8,128)} async-done(((f32[5760,256]{1,0:T(8,128)}), f32[5760,256]{1,0:T(8,128)}) %all-reduce.26.cloned.1.call-update) | async-done | bytes 5898256 | tf_op jit(solution)/shard_map/psum | solution.py:19
  1102.8 25.7 %convolution_bitcast_fusion.7 = f32[4096,256]{0,1:T(8,128)} fusion(bf16[5760,4096]{1,0:T(8,128)(2,1)} %param.6, f32[5760,256]{1,0:T(8,128)} %param.8, f32[5760,256]{1,0:T(8,128)} %all-reduce.26.cloned.1.call-done, f32[5760]{0:T(1024)S(1)} %copy-done.3), kind=kOutput, calls=%fused_computation.19 | convolution fusion | flops 12084019200 | bytes 63199744 | tf_op jit(solution)/shard_map/dot_general | solution.py:22
  1128.8 154.0 %all-reduce.28.cloned.1.call-done = f32[4096,256]{0,1:T(8,128)} async-done(((f32[4096,256]{0,1:T(8,128)}), f32[4096,256]{0,1:T(8,128)}) %all-reduce.28.cloned.1.call-update) | async-done | bytes 4194320 | tf_op jit(solution)/shard_map/psum | solution.py:23
  1282.8 5.9 multiply_add_fusion.2
  1290.7 21.5 %convolution_bitcast_fusion.1 = f32[5760,256]{1,0:T(8,128)} fusion(bf16[5760,4096]{1,0:T(8,128)(2,1)} %param.6, f32[4096,256]{0,1:T(8,128)S(1)} %multiply_add_fusion.2), kind=kOutput, calls=%fused_computation.1 | convolution fusion | flops 12080644096 | bytes 57278464 | tf_op jit(solution)/shard_map/dot_general | solution.py:18
  1312.2 112.1 %all-reduce.30.cloned.1.call-done = f32[5760,256]{1,0:T(8,128)} async-done(((f32[5760,256]{1,0:T(8,128)}), f32[5760,256]{1,0:T(8,128)}) %all-reduce.30.cloned.1.call-update) | async-done | bytes 5898256 | tf_op jit(solution)/shard_map/psum | solution.py:19
  1424.3 25.8 %convolution_bitcast_fusion.6 = f32[4096,256]{0,1:T(8,128)} fusion(bf16[5760,4096]{1,0:T(8,128)(2,1)} %param.6, f32[5760,256]{1,0:T(8,128)} %param.8, f32[5760,256]{1,0:T(8,128)} %all-reduce.30.cloned.1.call-done, f32[5760]{0:T(1024)S(1)} %copy-done.3), kind=kOutput, calls=%fused_computation.18 | convolution fusion | flops 12084019200 | bytes 63199744 | tf_op jit(solution)/shard_map/dot_general | solution.py:22
  1450.4 153.9 %all-reduce.32.cloned.1.call-done = f32[4096,256]{0,1:T(8,128)} async-done(((f32[4096,256]{0,1:T(8,128)}), f32[4096,256]{0,1:T(8,128)}) %all-reduce.32.cloned.1.call-update) | async-done | bytes 4194320 | tf_op jit(solution)/shard_map/psum | solution.py:23
  1604.3 25.0 %convolution_bitcast_fusion = f32[5760,256]{1,0:T(8,128)} fusion(bf16[5760,4096]{1,0:T(8,128)(2,1)} %param.6, f32[4096,256]{0,1:T(8,128)} %copy-done.1, f32[4096,256]{0,1:T(8,128)} %all-reduce.32.cloned.1.call-done, f32[4096]{0:T(1024)S(1)} %broadcast_multiply_fusion), kind=kOutput, calls=%fused_computation | convolution fusion | flops 12082741248 | bytes 61489152 | tf_op jit(solution)/shard_map/dot_general | solution.py:18
  1629.4 112.1 %all-reduce.34.cloned.1.call-done = f32[5760,256]{1,0:T(8,128)} async-done(((f32[5760,256]{1,0:T(8,128)}), f32[5760,256]{1,0:T(8,128)}) %all-reduce.34.cloned.1.call-update) | async-done | bytes 5898256 | tf_op jit(solution)/shard_map/psum | solution.py:19
  1741.5 14.8 multiply_reduce_fusion.1
  1756.3 2.6 copy-done
  1758.9 22.2 %convolution_bitcast_fusion.5 = f32[4096,256]{0,1:T(8,128)} fusion(bf16[5760,4096]{1,0:T(8,128)(2,1)} %param.6, f32[5760,256]{1,0:T(8,128)S(1)} %get-tuple-element.20), kind=kOutput, calls=%fused_computation.17 | convolution fusion | flops 12081070080 | bytes 57278464 | tf_op jit(solution)/shard_map/dot_general | solution.py:22
  1781.1 12.2 all-reduce
  1794.0 141.4 %all-reduce.36.cloned.1.call-done = f32[4096,256]{0,1:T(8,128)} async-done(((f32[4096,256]{0,1:T(8,128)}), f32[4096,256]{0,1:T(8,128)}) %all-reduce.36.cloned.1.call-update) | async-done | bytes 4194320 | tf_op jit(solution)/shard_map/psum | solution.py:23
  1935.5 8.2 multiply_add_fusion
  1943.6 5.6 copy.15
  (38 shorter events, 6.6 us)
Async XLA Ops:
  7.2 139.6 %all-reduce.14.cloned.1.call-start = ((), (), s32[]{:S(2)}) async-start(), calls=%async_computation | async-start | bytes 11796480 | tf_op jit(solution)/shard_map/psum | solution.py:19
  30.9 115.9 %copy-start.3 = (f32[5760]{0:T(1024)S(1)}, f32[5760]{0:T(1024)}, u32[]{:S(2)}) copy-start(f32[5760]{0:T(1024)} %param.9) | copy-start | bytes 69124
  30.9 295.9 %all-reduce.16.cloned.1.call-start = ((), (), s32[]{:S(2)}) async-start(), calls=%async_computation.1 | async-start | bytes 8388608 | tf_op jit(solution)/shard_map/psum | solution.py:23
  172.6 6.5 copy-start.4
  172.6 291.4 %all-reduce.18.cloned.1.call-start = ((), (), s32[]{:S(2)}) async-start(), calls=%async_computation.2 | async-start | bytes 11796480 | tf_op jit(solution)/shard_map/psum | solution.py:19
  351.9 292.1 %all-reduce.20.cloned.1.call-start = ((), (), s32[]{:S(2)}) async-start(), calls=%async_computation.3 | async-start | bytes 8388608 | tf_op jit(solution)/shard_map/psum | solution.py:23
  489.8 295.7 %all-reduce.22.cloned.1.call-start = ((), (), s32[]{:S(2)}) async-start(), calls=%async_computation.4 | async-start | bytes 11796480 | tf_op jit(solution)/shard_map/psum | solution.py:19
  649.9 2.0 copy-start.2
  673.4 292.2 %all-reduce.24.cloned.1.call-start = ((), (), s32[]{:S(2)}) async-start(), calls=%async_computation.5 | async-start | bytes 8388608 | tf_op jit(solution)/shard_map/psum | solution.py:23
  811.4 291.4 %all-reduce.26.cloned.1.call-start = ((), (), s32[]{:S(2)}) async-start(), calls=%async_computation.6 | async-start | bytes 11796480 | tf_op jit(solution)/shard_map/psum | solution.py:19
  990.6 292.1 %all-reduce.28.cloned.1.call-start = ((), (), s32[]{:S(2)}) async-start(), calls=%async_computation.7 | async-start | bytes 8388608 | tf_op jit(solution)/shard_map/psum | solution.py:23
  1128.6 295.8 %all-reduce.30.cloned.1.call-start = ((), (), s32[]{:S(2)}) async-start(), calls=%async_computation.8 | async-start | bytes 11796480 | tf_op jit(solution)/shard_map/psum | solution.py:19
  1288.6 2.0 copy-start.1
  1312.2 292.2 %all-reduce.32.cloned.1.call-start = ((), (), s32[]{:S(2)}) async-start(), calls=%async_computation.9 | async-start | bytes 8388608 | tf_op jit(solution)/shard_map/psum | solution.py:23
  1450.1 291.4 %all-reduce.34.cloned.1.call-start = ((), (), s32[]{:S(2)}) async-start(), calls=%async_computation.10 | async-start | bytes 11796480 | tf_op jit(solution)/shard_map/psum | solution.py:19
  1629.4 306.1 %all-reduce.36.cloned.1.call-start = ((), (), s32[]{:S(2)}) async-start(), calls=%async_computation.11 | async-start | bytes 8388608 | tf_op jit(solution)/shard_map/psum | solution.py:23
  1756.3 2.6 copy-start
Sparse Core Ops, SparseCore 0:
  31.0 115.7 all-reduce.13
  172.8 154.0 all-reduce.15
  352.0 112.0 all-reduce.17
  489.9 154.0 all-reduce.19
  673.5 112.0 all-reduce.21
  811.5 154.0 all-reduce.23
  990.8 112.0 all-reduce.25
  1128.7 154.0 all-reduce.27
  1312.3 111.9 all-reduce.29
  1450.2 154.0 all-reduce.31
  1629.5 111.9 all-reduce.33
  1781.2 154.1 all-reduce.35
where the time goes:
time: 1960 us
  waiting for transfers between devices  1580 us (81%)
  matrix products  293 us (15%)
  other arithmetic  34.7 us (2%)
    psum x6, waiting for transfers between devices, local_sweeps(): back_proj = lax.psum(part_back, 'ray')  905 us
    psum x6, waiting for transfers between devices, local_sweeps(): projected = lax.psum(part_proj, 'pix')  676 us
    dot_general x6, matrix products, local_sweeps(): lax.dot_general(a_blk, residual.astype(jnp.bfloat16), (((0,), (0,)), ((),...  151 us
    dot_general x6, matrix products, local_sweeps(): jnp.dot(a_blk, x_cur.astype(jnp.bfloat16), preferred_element_type=jnp.flo...  142 us
  transfers between devices with their start and end apart: 12, of which 12 were waited for; matrix products, arithmetic and copies ran while one was open for 0% of the time, Pallas kernels for 0%

commit v1 on v0

v1 whole, which is shorter than its diff:
```python
import functools

import jax
import jax.numpy as jnp
from jax import lax
from jax.experimental import pallas as pl
from jax.experimental.pallas import tpu as pltpu
from jax.sharding import PartitionSpec as P

SWEEPS = 6
MESH = pl.DeviceIdType.MESH
NR = 9
NP = 16
HP = NP // 2
L1, L2, L3, L4 = 1, 2, 4, 5
RL, AL = 2, 2
FSLOTS = NR + L4
ZSLOTS = HP + 3 * RL + 3 * AL
PERIOD = FSLOTS + ZSLOTS
OFFSET = PERIOD // 2
TOTAL = PERIOD * SWEEPS + OFFSET


def sweep_kernel(a_hbm, xb_hbm, x_hbm, sino, rinv, lamcol, x_out, r_out, sq_out,
                 a_v, pbuf, crecv, yrecv, rt, gbuf, zrecv, xf, xb,
                 a_sem, in_sem, crs_s, crs_r, yrs_s, yrs_r, yag_s, yag_r, cag_s, cag_r,
                 zrs_s, zrs_r, zag_s, zag_r, ry_s, ry_r, rc_s, rc_r, rout_sem, xout_sem):
    part, z, pix = lax.axis_index("part"), lax.axis_index("ray"), lax.axis_index("pix")
    y, core = pix // 2, lax.rem(pix, 2)
    partner = (part, z, y * 2 + (1 - core))
    yneigh = (part, z, (1 - y) * 2 + core)
    zlow = (part, jnp.maximum(z - 1, 0), pix)
    zhigh = (part, jnp.minimum(z + 1, 3), pix)
    rows = a_v.shape[0] // NR
    mine64 = pl.ds(pl.multiple_of(core * 64, 64), 64)
    other64 = pl.ds(pl.multiple_of((1 - core) * 64, 64), 64)
    own32 = pl.ds(pl.multiple_of(core * 64 + y * 32, 32), 32)
    nb32 = pl.ds(pl.multiple_of(core * 64 + (1 - y) * 32, 32), 32)

    def a_copy(i):
        sl = pl.ds(pl.multiple_of(i * rows, rows), rows)
        return pltpu.make_async_copy(a_hbm.at[sl], a_v.at[sl], a_sem.at[i])

    half_off = jnp.where(z >= 2, HP, 0)
    xb_copy = pltpu.make_async_copy(xb_hbm, xb, in_sem.at[0])
    xf_copy = pltpu.make_async_copy(x_hbm.at[:, pl.ds(half_off, HP)], xf, in_sem.at[1])
    xb_copy.start()
    for i in range(NR):
        a_copy(i).start()
    xf_copy.start()

    barrier = pltpu.get_barrier_semaphore()
    pl.semaphore_signal(barrier, inc=1, device_id=partner, device_id_type=MESH)
    pl.semaphore_signal(barrier, inc=1, device_id=yneigh, device_id_type=MESH)

    @pl.when(z > 0)
    def _():
        pl.semaphore_signal(barrier, inc=1, device_id=zlow, device_id_type=MESH)

    @pl.when(z < 3)
    def _():
        pl.semaphore_signal(barrier, inc=1, device_id=zhigh, device_id_type=MESH)

    middle = jnp.logical_and(z > 0, z < 3)

    @pl.when(middle)
    def _():
        pl.semaphore_wait(barrier, 4)

    @pl.when(jnp.logical_not(middle))
    def _():
        pl.semaphore_wait(barrier, 3)

    sq_out[...] = jnp.zeros_like(sq_out)
    xb_copy.wait()
    xf_copy.wait()

    def remote(src, dst, ssem, rsem, dev):
        return pltpu.make_async_remote_copy(
            src_ref=src, dst_ref=dst, send_sem=ssem, recv_sem=rsem, device_id=dev, device_id_type=MESH)

    def core_rs(i):
        return remote(pbuf.at[i, other64], crecv.at[i], crs_s.at[i], crs_r.at[i], partner)

    def y_rs(i):
        return remote(pbuf.at[i, nb32], yrecv.at[i], yrs_s.at[i], yrs_r.at[i], yneigh)

    def y_ag(i, buf):
        return remote(buf.at[i, own32], buf.at[i, own32], yag_s.at[i], yag_r.at[i], yneigh)

    def core_ag(i, buf, which):
        sl = own32 if which == 0 else nb32
        return remote(buf.at[i, sl], buf.at[i, sl], cag_s.at[which, i], cag_r.at[which, i], partner)

    def r_local(h, i):
        return pltpu.make_async_copy(pbuf.at[i, own32], r_out.at[h, i, own32], rout_sem.at[i])

    def r_y(h, i):
        return remote(pbuf.at[i, own32], r_out.at[h, i, own32], ry_s.at[i], ry_r.at[i], yneigh)

    def r_core(h, i, which):
        if which == 0:
            src, dst = pbuf.at[i, own32], r_out.at[h, i, own32]
        else:
            src, dst = r_out.at[h, i, nb32], r_out.at[h, i, nb32]
        return remote(src, dst, rc_s.at[which, i], rc_r.at[which, i], partner)

    def x_local(h, c, j):
        return pltpu.make_async_copy(xf.at[h, c], x_out.at[h, j], xout_sem.at[h, c])

    def on(i, n, body):
        pl.when(jnp.logical_and(i >= 0, i < n))(body)

    def z_rs(h, j, dev):
        return remote(gbuf.at[h, j], zrecv.at[j], zrs_s.at[h, j], zrs_r.at[h, j], dev)

    def z_ag(h, j, buf, dev):
        return remote(buf.at[h, j], buf.at[h, j], zag_s.at[h, j], zag_r.at[h, j], dev)

    def by_kind(last, low, high, body):
        @pl.when(jnp.logical_not(last))
        def _():
            body(low)

        @pl.when(last)
        def _():
            body(high)

    def step1(h, v):
        i = v - L1

        def body():
            copy = core_rs(i)
            copy.wait_recv()
            pbuf[i, mine64] += crecv[i]
            y_rs(i).start()
            copy.wait_send()

        on(i, NR, body)

    def forward(h, k, v):
        i = v

        def body():
            if h == 0:
                @pl.when(k == 0)
                def _():
                    a_copy(i).wait()
            xv = jnp.concatenate([xb[h, j] for j in range(NP)], axis=1)
            av = a_v[pl.ds(pl.multiple_of(i * rows, rows), rows), :]
            pbuf[i] = lax.dot_general(xv, av, (((1,), (1,)), ((), ())), preferred_element_type=jnp.float32)
            core_rs(i).start()

        on(i, NR, body)

    def step2(h, k, v, last):
        i = v - L2

        def body():
            copy = y_rs(i)
            copy.wait_recv()
            resid = rinv[i] * (sino[h, i] - (pbuf[i, own32] + yrecv[i]))
            sqr = resid * resid
            fold = sqr[:, :128]
            for t in range(1, rows // 128):
                fold = fold + sqr[:, t * 128:(t + 1) * 128]
            sq_out[k, pl.ds(h * 32, 32)] += fold

            rt[i, own32] = resid.astype(jnp.bfloat16)
            y_ag(i, rt).start()
            core_ag(i, rt, 0).start()

            @pl.when(last)
            def _():
                pbuf[i, own32] = resid
                r_y(h, i).start()
                r_core(h, i, 0).start()
                r_local(h, i).start()

            copy.wait_send()

        on(i, NR, body)

    def step3(h, v, last):
        i = v - L3

        def body():
            remote(rt.at[i, nb32], rt.at[i, nb32], yag_s.at[i], yag_r.at[i], yneigh).wait_recv()
            core_ag(i, rt, 1).start()

            @pl.when(last)
            def _():
                remote(r_out.at[h, i, nb32], r_out.at[h, i, nb32], ry_s.at[i], ry_r.at[i], yneigh).wait_recv()
                r_core(h, i, 1).start()

        on(i, NR, body)

    def backward(h, v, last):
        i = v - L4

        def body():
            for which in (0, 1):
                core_ag(i, rt, which).wait_recv()
            rv = rt[i]
            sl = pl.ds(pl.multiple_of(i * rows, rows), rows)

            width = gbuf.shape[3]
            for j in range(NP):
                lanes = pl.ds(j * width, width)
                prod = jnp.dot(rv, a_v[sl, lanes], preferred_element_type=jnp.float32)
                gbuf[h, j] = jnp.where(i == 0, prod, gbuf[h, j] + prod)

            y_ag(i, rt).wait_send()
            for which in (0, 1):
                core_ag(i, rt, which).wait_send()

            @pl.when(last)
            def _():
                r_y(h, i).wait_send()
                r_local(h, i).wait()
                for which in (0, 1):
                    r_core(h, i, which).wait_recv()
                    r_core(h, i, which).wait_send()

        on(i, NR, body)

    def z_steps(h, v, last):
        zt = v - FSLOTS
        for direction in (0, 1):
            if direction == 0:
                d, down, up = 3 - z, zlow, zhigh
            else:
                d, down, up = z, zhigh, zlow
            base = direction * HP

            def reduce(d=d, down=down, up=up, base=base):
                c = zt - RL * d
                j = base + c

                @pl.when(d > 0)
                def _():
                    z_rs(h, j, down).wait_recv()
                    gbuf[h, j] += zrecv[j]

                @pl.when(d < 3)
                def _():
                    z_rs(h, j, down).start()

                @pl.when(d == 3)
                def _():
                    new = xf[h, c] + lamcol[j] * gbuf[h, j]

                    @pl.when(jnp.logical_not(last))
                    def _():
                        xf[h, c] = new
                        xb[h, j] = new.astype(jnp.bfloat16)
                        z_ag(h, j, xb, up).start()

                    @pl.when(last)
                    def _():
                        xf[h, c] = new
                        x_local(h, c, j).start()
                        remote(xf.at[h, c], x_out.at[h, j], zag_s.at[h, j], zag_r.at[h, j], up).start()

            on(zt - RL * d, HP, reduce)

            def spread(d=d, down=down, up=up, base=base):
                j = base + zt - 3 * RL - AL * (3 - d)

                def kind(buf):
                    z_ag(h, j, buf, up).wait_recv()

                    @pl.when(d > 0)
                    def _():
                        z_ag(h, j, buf, up).start()

                z_rs(h, j, down).wait_send()
                by_kind(last, xb, x_out, kind)

            @pl.when(d < 3)
            def _(spread=spread, d=d):
                on(zt - 3 * RL - AL * (3 - d), HP, spread)

            def sent(d=d, up=up, base=base):
                c = zt - 3 * RL - AL * (4 - d)
                j = base + c

                def kind(buf):
                    z_ag(h, j, buf, up).wait_send()

                by_kind(last, xb, x_out, kind)

                @pl.when(jnp.logical_and(last, d == 3))
                def _():
                    x_local(h, c, j).wait()

            @pl.when(d > 0)
            def _(sent=sent, d=d):
                on(zt - 3 * RL - AL * (4 - d), HP, sent)

    def slot(t, _):
        state = []
        for h in (0, 1):
            u = t - h * OFFSET
            k = u // PERIOD
            v = u - k * PERIOD
            active = jnp.logical_and(u >= 0, k < SWEEPS)
            v = jnp.where(active, v, -1000)
            k = jnp.clip(k, 0, SWEEPS - 1)
            state.append((h, k, v, k == SWEEPS - 1))
        for h, k, v, last in state:
            @pl.when(jnp.logical_and(v >= 0, v < FSLOTS))
            def _(h=h, v=v):
                step1(h, v)
        for h, k, v, last in state:
            @pl.when(v >= FSLOTS)
            def _(h=h, v=v, last=last):
                z_steps(h, v, last)
        for h, k, v, last in state:
            @pl.when(jnp.logical_and(v >= 0, v < FSLOTS))
            def _(h=h, k=k, v=v, last=last):
                forward(h, k, v)
                step2(h, k, v, last)
                step3(h, v, last)
                backward(h, v, last)
        return 0

    lax.fori_loop(0, TOTAL, slot, 0)


def solution(mesh):
    ray_size = mesh.shape["ray"]

    def local_sweeps(a_blk, x_loc, sino_loc, row_inv, col_inv, relaxation):
        rays, pixels = a_blk.shape
        cols = x_loc.shape[1]
        rows, lanes = rays // NR, pixels // NP
        pix = lax.axis_index("pix")
        q = lax.rem(pix, 2) * 2 + pix // 2
        x0 = x_loc.reshape(NP, lanes, 2, 128).transpose(2, 0, 3, 1)
        own = lax.dynamic_slice_in_dim(sino_loc.reshape(NR, rows, 2, 4, 32), q, 1, axis=3)
        sino = own.reshape(NR, rows, 2, 32).transpose(2, 0, 3, 1)
        rinv = row_inv.reshape(NR, 1, rows)
        lamcol = (relaxation * col_inv).reshape(NP, 1, lanes)
        f32, bf16 = jnp.float32, jnp.bfloat16
        dma = pltpu.SemaphoreType.DMA
        anyspace = pl.BlockSpec(memory_space=pl.ANY)
        vmem = pl.BlockSpec(memory_space=pltpu.VMEM)
        x_new, r_new, sq = pl.pallas_call(
            sweep_kernel,
            out_shape=(
                jax.ShapeDtypeStruct((2, NP, 128, lanes), f32),
                jax.ShapeDtypeStruct((2, NR, 128, rows), f32),
                jax.ShapeDtypeStruct((SWEEPS, 64, 128), f32),
            ),
            in_specs=[anyspace, anyspace, anyspace, vmem, vmem, vmem],
            out_specs=(anyspace, anyspace, vmem),
            scratch_shapes=[
                pltpu.VMEM((rays, pixels), bf16),
                pltpu.VMEM((NR, 128, rows), f32),
                pltpu.VMEM((NR, 64, rows), f32),
                pltpu.VMEM((NR, 32, rows), f32),
                pltpu.VMEM((NR, 128, rows), bf16),
                pltpu.VMEM((2, NP, 128, lanes), f32),
                pltpu.VMEM((NP, 128, lanes), f32),
                pltpu.VMEM((2, HP, 128, lanes), f32),
                pltpu.VMEM((2, NP, 128, lanes), bf16),
                dma((NR,)), dma((2,)),
                dma((NR,)), dma((NR,)), dma((NR,)), dma((NR,)), dma((NR,)), dma((NR,)),
                dma((2, NR)), dma((2, NR)),
                dma((2, NP)), dma((2, NP)), dma((2, NP)), dma((2, NP)),
                dma((NR,)), dma((NR,)), dma((2, NR)), dma((2, NR)),
                dma((NR,)), dma((2, HP)),
            ],
            compiler_params=pltpu.CompilerParams(
                collective_id=0, has_side_effects=True, vmem_limit_bytes=67043328),
        )(a_blk, x0.astype(bf16), x0, sino, rinv, lamcol)
        x_fin = x_new.transpose(1, 3, 0, 2).reshape(pixels, cols)
        resid = r_new.transpose(1, 3, 0, 2).reshape(rays, cols)
        sums = jnp.sum(sq, axis=-1).reshape(SWEEPS, 2, 1, 32)
        spread = jnp.where(jnp.arange(4)[None, None, :, None] == q, sums, 0.0).reshape(SWEEPS, cols)
        sq_norms = lax.psum(spread, ("ray", "pix")) / (rays * ray_size)
        return x_fin, resid, sq_norms

    return jax.shard_map(
        local_sweeps,
        mesh=mesh,
        in_specs=(P("ray", "pix"), P("pix", "part"), P("ray", "part"), P("ray"), P("pix"), P()),
        out_specs=(P("pix", "part"), P("ray", "part"), P(None, "part")),
        check_vma=False,
    )
```

time: 1960 us -> 758 us (0.39)
  waiting for transfers between devices: 1580 us -> 0 us
  Pallas kernels: 0 us -> 659 us
  matrix products: 293 us -> 0 us
  local copies, waits for them, and re-layouts: 18.4 us -> 60.5 us
  other arithmetic: 34.7 us -> 5.15 us
    psum x12 -> x0, waiting for transfers between devices: 1580 us -> none  [the longest x6 905 us: local_sweeps(): back_proj = lax.psum(part_back, 'ray')]
    pallas_call x0 -> x1, Pallas kernels: none -> 659 us  [local_sweeps(): pl.pallas_call(sweep_kernel, out_shape=(jax.ShapeDtypeStruct((2, NP, 128,...]
    dot_general x12 -> x0, matrix products: 293 us -> none  [the longest x6 151 us: local_sweeps(): lax.dot_general(a_blk, residual.astype(jnp.bfloat16), (((0,), (0,)), ((),...]
    reshape x0 -> x4, local copies, waits for them, and re-layouts: none -> 21.3 us  [the longest x2 12.9 us: local_sweeps(): x0 = x_loc.reshape(NP, lanes, 2, 128).transpose(2, 0, 3, 1)]
    add x3 -> x0, other arithmetic: 19.9 us -> none  [local_sweeps(): x_cur = x_cur + relaxation * col_inv[:, None] * back_proj]
  transfers between devices with their start and end apart: 12 -> 0, of which waited for: 12 -> 0; matrix products, arithmetic and copies ran while one was open for 0% -> 0% of each run, Pallas kernels for 0% -> 0%
where the time goes in v1:
time: 758 us; the launch traced here: 757 us
  Pallas kernels  659 us (87%)
  local copies, waits for them, and re-layouts  60.5 us (8%)
  blocking collectives  30.7 us (4%)
    pallas_call x1, Pallas kernels, local_sweeps(): pl.pallas_call(sweep_kernel, out_shape=(jax.ShapeDtypeStruct((2, NP, 128,...  659 us
    psum x1, blocking collectives, local_sweeps(): sq_norms = lax.psum(spread, ('ray', 'pix')) / (rays * ray_size)  30.7 us
    unnamed x10, local copies, waits for them, and re-layouts  23.8 us

profile of v1, /device:TPU:0, one launch (start us, length us, event | category | flops | bytes accessed | tf_op | source)
XLA Modules:
  0.0 756.7 jit_solution(548532718432191052)
XLA Ops:
  0.7 6.4 copy.12
  7.0 7.8 %reshape.38 = f32[9,640,2,4,32]{1,0,4,3,2:T(8,128)} reshape(f32[5760,256]{0,1:T(8,128)} %copy.12) | data formatting | bytes 11796480 | tf_op jit(solution)/shard_map/reshape | solution.py:341
  14.8 1.9 constant_dynamic-slice_fusion
  16.7 1.6 copy.28
  18.3 5.7 reshape.44
  24.1 7.2 copy.11
  31.2 0.0 copy-start.1
  31.2 0.0 copy-start.2
  31.2 3.8 bitcast_convert_fusion.xb_hbm
  35.1 0.0 copy-done.1
  35.1 0.6 reshape.40.rinv
  36.3 0.0 copy-done.2
  36.3 0.6 broadcast_multiply_fusion
  36.9 659.1 %shard_map.85 = (f32[2,16,128,256]{3,2,1,0:T(8,128)}, f32[2,9,128,640]{3,2,1,0:T(8,128)}, f32[6,64,128]{2,1,0:T(8,128)}) custom-call(bf16[5760,4096]{1,0:T(8,128)(2,1)} %a_hbm.1, bf16[2,16,128,256]{3,2,1,0:T(8,128)(2,1)} %bitcast_convert_fusion.xb_hbm, f32[2,16,128,256]{3,2,1,0:T(8,128)} %bitcast.22, f32[2,9,32,640]{3,2,1,0:T(8,128)} %bitcast.27, ...), custom_call_target="tpu_custom_call" | custom-call | tf_op jit(solution)/shard_map/pallas_call | solution.py:349
  696.0 11.6 %copy.15 = f32[9,640,2,128]{3,2,1,0:T(2,128)} copy(f32[9,640,2,128]{1,3,0,2:T(8,128)} %bitcast.26) | data formatting | bytes 11796480 | tf_op jit(solution)/shard_map/transpose | solution.py:379
  707.6 5.6 copy.26
  713.2 7.2 copy.19
  720.4 0.0 copy-start
  720.4 4.5 copy.27
  724.9 0.0 copy-done
  724.9 0.1 reduce_sum.9
  725.1 0.1 broadcast_in_dim.32
  725.1 0.1 broadcast_in_dim.34
  725.2 0.1 broadcast_in_dim.29
  725.3 0.1 broadcast_in_dim.30
  725.4 30.7 %psum.7 = f32[6,256]{1,0:T(8,128)S(1)} all-reduce(f32[6,256]{1,0:T(8,128)S(1)} %broadcast_select_fusion), channel_id=1, replica_groups=mesh['part'=2,'ray'=4,'pix'=4] {'ray','pix'}, use_global_device_ids=true, to_apply=%region_1.2 | all-reduce | flops 1536 | bytes 12288 | tf_op jit(solution)/shard_map/psum | solution.py:382
  756.1 0.6 broadcast_multiply_fusion.1
  (3 shorter events, 0.0 us)
Async XLA Ops:
  31.2 3.8 copy-start.1
  31.2 5.1 copy-start.2
  720.4 4.5 copy-start
